TPU v7x, 256 devices: a whole 4x4x8 slice. The times are simulated.
256 devices in a mesh: rp: 64 (over y, x, z_hi, core), re: 4 (over z_lo).
Axes of the slice: x: 4, y: 4, z: 8 (z_hi: 2, z_lo: 4; z = z_hi * 4 + z_lo), core: 2. Of those that a mesh axis runs over, the one named last changes fastest.
Arguments:
- coupling: bfloat16 [1024, 4, 2, 6, 4096], P('rp', 're'), may hold values from -0.4375 to 0.4375
- rp_coords: int32 [3, 1024], P(None, 'rp'), may hold values from -8 to 8
- degeneracy: int32 [1024], P('rp'), may hold values from 1 to 8
- qpoints: int32 [3, 512], replicated, may hold values from 0 to 15
- eigvec: float32 [512, 2, 6, 6], P('rp'), may hold values from -1.75 to 1.75
Outputs:
- coupling_q: float32 [512, 4, 2, 6, 4096], P('rp', None, None, None, 're')
All inputs are finite; a program needn't handle non-finite values.
Results may differ from a plain program's by a relative error of at most 0.0042.
Values may be sent and summed in bfloat16 or wider, within the bound.
A program may use at most 64 MiB of HBM per device.

v0:
```python
import math

import jax
import jax.numpy as jnp
from jax import lax
from jax.sharding import PartitionSpec as P

QGRID = 16


def laid_out(tiles, dim):
    dims = list(tiles.shape[1:])
    dims[dim] *= tiles.shape[0]
    return jnp.moveaxis(tiles, 0, dim).reshape(dims)


def from_everyone(x, axis):
    peers = lax.axis_size(axis)
    return lax.all_to_all(jnp.broadcast_to(x[None], (peers, *x.shape)), axis, 0, 0, tiled=True)


def gathered_copies(x, axis, dim):
    return laid_out(from_everyone(x, axis), dim)


def in_blocks(x, dim, peers):
    before, after = (x.shape[:dim], x.shape[dim + 1 :])
    return jnp.moveaxis(x.reshape(*before, peers, -1, *after), dim, 0)


def joined_exchange(x, axis, axes, splits, concats):
    sizes = [lax.axis_size(a) for a in axes]
    tiles = in_blocks(x, splits[0], sizes[0])
    tiles = jnp.moveaxis(in_blocks(tiles, splits[1] + 1, sizes[1]), 0, 1)
    inside = tiles.shape[2:]
    tiles = tiles.reshape(-1, *inside)
    tiles = lax.all_to_all(tiles, axis, split_axis=0, concat_axis=0, tiled=True)
    tiles = laid_out(tiles.reshape(*sizes, *inside), concats[0] + 1)
    return laid_out(tiles, concats[1])


def phases(points, coords, degeneracy):
    turns = jnp.mod(points[0][:, None] * coords[0][None, :], QGRID)
    turns = turns + jnp.mod(points[1][:, None] * coords[1][None, :], QGRID)
    turns = turns + jnp.mod(points[2][:, None] * coords[2][None, :], QGRID)
    turns = jnp.mod(turns, QGRID)
    angles = turns.astype(jnp.float32) * (2.0 * math.pi / QGRID)
    weights = 1.0 / degeneracy.astype(jnp.float32)
    table = jnp.concatenate(
        [jnp.cos(angles) * weights[None, :], jnp.sin(angles) * weights[None, :]], axis=0
    )
    return table.astype(jnp.bfloat16)


def combine(table, coupling):
    point_count = table.shape[0] // 2
    product = jnp.dot(
        table, coupling.reshape(coupling.shape[0], -1), preferred_element_type=jnp.float32
    )
    product = product.reshape((2, point_count) + coupling.shape[1:])
    real_part = product[0, :, :, 0] - product[1, :, :, 1]
    imag_part = product[0, :, :, 1] + product[1, :, :, 0]
    return jnp.stack([real_part, imag_part], axis=2)


def mode_mix(values, matrix):
    return jnp.einsum("qrkp,qkn->qrnp", values, matrix, precision=lax.Precision.HIGHEST)


def rotate(summed, eigvec):
    real_in = summed[:, :, 0]
    imag_in = summed[:, :, 1]
    vec_real = eigvec[:, 0]
    vec_imag = eigvec[:, 1]
    real_out = mode_mix(real_in, vec_real) - mode_mix(imag_in, vec_imag)
    imag_out = mode_mix(real_in, vec_imag) + mode_mix(imag_in, vec_real)
    return jnp.stack([real_out, imag_out], axis=2)


def to_owners(all_points):
    return lax.all_to_all(
        all_points.astype(jnp.bfloat16), "rp", split_axis=0, concat_axis=3, tiled=True
    ).astype(all_points.dtype)


def per_device(coupling, rp_coords, degeneracy, qpoints, eigvec):
    stacked = jnp.concatenate([rp_coords, degeneracy[None, :]], axis=0)
    lattice = gathered_copies(stacked, "rp", 1)
    table = phases(qpoints, lattice[:3], lattice[3])
    rp_count = lax.axis_size("rp")
    re_count = lax.axis_size("re")
    local_rp, local_re, parts, mode_count, pair_count = coupling.shape
    q_local = eigvec.shape[0]
    pair_share = pair_count // re_count
    block_cols = mode_count * pair_share
    inner = block_cols // rp_count
    reordered = coupling.reshape(local_rp, local_re, parts, mode_count, re_count, pair_share)
    reordered = jnp.swapaxes(reordered, 3, 4)
    reordered = reordered.reshape(local_rp, local_re, parts, re_count, rp_count, inner)
    reordered = jnp.swapaxes(reordered, 3, 4)
    reordered = reordered.reshape(local_rp, local_re, parts, rp_count * re_count * inner)
    moved = joined_exchange(reordered, ("rp", "re"), ("rp", "re"), (3, 3), (0, 1))
    all_points = combine(table, moved)
    summed = to_owners(all_points)
    summed = summed.reshape(q_local, summed.shape[1], parts, mode_count, pair_share)
    return rotate(summed, eigvec)


def solution(mesh):
    return jax.shard_map(
        per_device,
        mesh=mesh,
        in_specs=(
            P("rp", "re", None, None, None),
            P(None, "rp"),
            P("rp"),
            P(),
            P("rp", None, None, None),
        ),
        out_specs=P("rp", None, None, None, "re"),
        check_vma=False,
    )
```

profile of v0, /device:TPU:33, one launch (start us, length us, event | category | flops | bytes accessed | tf_op | source)
XLA Modules:
  0.0 161.4 jit_solution(17689326410087397459)
XLA Ops:
  0.0 0.7 pad_add_fusion
  0.7 0.7 broadcast_in_dim.5
  1.4 13.9 %all-to-all-start = ((s32[64,4,16]{2,1,0:T(4,128)}), s32[64,4,16]{2,1,0:T(4,128)S(1)}, u32[]{:S(2)}, u32[]{:S(2)}) async-start(s32[64,4,16]{2,1,0:T(4,128)} %broadcast_in_dim.5), calls=%async_computation | async-start | bytes 262144 | tf_op jit(solution)/shard_map/all_to_all | solution.py:19
  15.3 3.7 %reshape.92 = bf16[16,1,2,6,4,1024]{5,4,2,3,0,1:T(4,128)(2,1)} reshape(bf16[16,1,2,6,4096]{4,2,3,1,0:T(2,128)(2,1)} %param.5) | data formatting | bytes 3145728 | tf_op jit(solution)/shard_map/reshape | solution.py:97
  19.0 2.5 %copy.68 = bf16[16,1,2,6,4,1024]{5,3,4,2,0,1:T(8,128)(2,1)S(1)} copy(bf16[16,1,2,6,4,1024]{5,4,2,3,0,1:T(4,128)(2,1)} %reshape.92) | data formatting | bytes 3145728 | tf_op jit(solution)/shard_map/reshape | solution.py:97
  21.5 3.5 %reshape.93 = bf16[16,1,2,4,64,96]{5,4,3,2,0,1:T(8,128)(2,1)} reshape(bf16[16,1,2,4,6,1024]{5,4,3,2,0,1:T(8,128)(2,1)S(1)} %bitcast.98) | data formatting | bytes 3145728 | tf_op jit(solution)/shard_map/reshape | solution.py:99
  25.0 4.9 %copy.42 = bf16[16,1,2,64,4,96]{5,4,3,2,0,1:T(4,128)(2,1)} copy(bf16[16,1,2,64,4,96]{5,3,4,2,0,1:T(8,128)(2,1)} %bitcast.101) | data formatting | bytes 3145728 | tf_op jit(solution)/shard_map/transpose | solution.py:100
  29.8 3.5 %reshape_reshape.6 = bf16[16,1,2,64,384]{4,3,2,0,1:T(8,128)(2,1)S(1)} reshape(bf16[16,1,2,64,4,96]{5,4,3,2,0,1:T(4,128)(2,1)} %copy.42) | data formatting | bytes 3145728 | tf_op jit(solution)/shard_map/reshape;reshape | solution.py:28
  33.3 0.6 fusion.25
  33.9 0.5 pad_maximum_fusion.1
  34.4 1.4 copy.43
  35.8 1.7 %copy.44 = bf16[256,16,1,2,96]{4,1,3,2,0:T(8,128)(2,1)} copy(bf16[256,16,1,2,96]{4,1,0,3,2:T(8,128)(2,1)S(1)} %bitcast.102) | data formatting | bytes 3145728 | tf_op jit(solution)/shard_map/reshape | solution.py:36
  37.5 0.0 copy-start.2
  37.5 0.0 all-to-all-done
  37.5 13.5 %all-to-all-start.1 = ((bf16[256,16,1,2,96]{4,1,3,2,0:T(8,128)(2,1)}), bf16[256,16,1,2,96]{4,1,3,2,0:T(8,128)(2,1)S(1)}, u32[]{:S(2)}, u32[]{:S(2)}) async-start(bf16[256,16,1,2,96]{4,1,3,2,0:T(8,128)(2,1)} %copy.44), calls=%async_computation.1 | async-start | bytes 4194304 | tf_op jit(solution)/shard_map/all_to_all | solution.py:37
  51.0 0.0 copy-done.2
  51.0 0.3 slice_reduce_fusion.2
  51.3 0.1 mul.73
  51.4 0.1 mul.78
  51.5 0.1 mul.83
  51.5 0.1 fusion.20
  51.7 0.1 div.15
  51.7 11.5 %multiply_convert_fusion.1 = (bf16[512,1024]{1,0:T(8,128)(2,1)S(1)}, bf16[512,1024]{1,0:T(8,128)(2,1)S(1)}) fusion(f32[1024]{0:T(1024)S(1)} %div.15, s32[1024]{0:T(1024)S(1)} %mul.83, s32[512]{0:T(512)S(1)} %bitcast.108, s32[1024]{0:T(1024)S(1)} %mul.78, s32[512]{0:T(512)S(1)} %bitcast.109, s32[1024]{0:T(1024)S(1)} %mul.73, s32[512]{0:T(512)S(1)} %bitcast.107), kind=kLoop, calls=%fused_computation.31 | loop fusion | flops 28835840 | bytes 2119680 | tf_op jit(solution)/shard_map/convert.4
  63.2 1.5 pad_maximum_fusion
  64.7 39.8 %all-to-all-done.1 = bf16[256,16,1,2,96]{4,1,3,2,0:T(8,128)(2,1)S(1)} async-done(((bf16[256,16,1,2,96]{4,1,3,2,0:T(8,128)(2,1)}), bf16[256,16,1,2,96]{4,1,3,2,0:T(8,128)(2,1)S(1)}, u32[]{:S(2)}, u32[]{:S(2)}) %all-to-all-start.1) | async-done | bytes 1572896 | tf_op jit(solution)/shard_map/all_to_all | solution.py:37
  104.5 0.0 copy-start
  104.5 1.3 copy-done
  105.8 2.0 %copy.45 = bf16[4,64,16,1,2,96]{5,2,1,4,0,3:T(8,128)(2,1)S(1)} copy(bf16[4,64,16,1,2,96]{5,2,4,0,1,3:T(8,128)(2,1)} %bitcast.100) | data formatting | bytes 3145728 | tf_op jit(solution)/shard_map/transpose | solution.py:14
  107.8 2.5 %copy.46 = bf16[1024,4,1,2,96]{0,4,3,1,2:T(8,128)(2,1)} copy(bf16[1024,4,1,2,96]{4,0,3,1,2:T(8,128)(2,1)S(1)} %bitcast.99) | data formatting | bytes 3145728 | tf_op jit(solution)/shard_map/transpose | solution.py:14
  110.3 3.9 %fusion.8 = f32[2,512,4,2,96]{1,4,3,2,0:T(8,128)S(1)} fusion(bf16[2,512,1024,1,1]{2,1,4,3,0:T(8,128)(2,1)} %bitcast.104, bf16[1024,4,1,2,96]{0,4,3,1,2:T(8,128)(2,1)} %copy.46), kind=kOutput, calls=%fused_computation.32 | convolution fusion | flops 1610612736 | bytes 6815744 | tf_op jit(solution)/shard_map/dot_general | solution.py:57
  114.1 0.1 fusion.17
  114.2 0.1 fusion.18
  114.3 0.1 pad_maximum_fusion.3
  114.4 0.0 copy-start.1
  114.4 1.4 copy.49
  115.9 4.9 %all-to-all-start.2 = ((bf16[512,4,2,96]{3,1,2,0:T(4,128)(2,1)}), bf16[512,4,2,96]{3,1,2,0:T(4,128)(2,1)S(1)}, u32[]{:S(2)}, u32[]{:S(2)}) async-start(bf16[512,4,2,96]{3,1,2,0:T(4,128)(2,1)} %copy.49), calls=%async_computation.2 | async-start | bytes 2097152 | tf_op jit(solution)/shard_map/all_to_all | solution.py:81
  120.8 0.0 copy-done.1
  120.9 0.1 copy.64
  121.0 0.1 copy.65
  121.1 33.1 %all-to-all-done.2 = bf16[512,4,2,96]{3,1,2,0:T(4,128)(2,1)S(1)} async-done(((bf16[512,4,2,96]{3,1,2,0:T(4,128)(2,1)}), bf16[512,4,2,96]{3,1,2,0:T(4,128)(2,1)S(1)}, u32[]{:S(2)}, u32[]{:S(2)}) %all-to-all-start.2) | async-done | bytes 786464 | tf_op jit(solution)/shard_map/all_to_all | solution.py:81
  154.2 0.1 copy.69
  154.4 0.3 copy.60
  154.7 1.8 %reshape.102 = bf16[8,4,2,6,1024]{4,3,1,0,2:T(8,128)(2,1)S(1)} reshape(bf16[8,4,2,64,96]{4,3,1,0,2:T(8,128)(2,1)S(1)} %copy.60) | data formatting | bytes 1572864 | tf_op jit(solution)/shard_map/reshape | solution.py:105
  156.4 0.6 fusion.16
  157.0 0.6 fusion.15
  157.6 0.6 fusion.11
  158.2 0.6 fusion.10
  158.8 0.2 pad_maximum_fusion.2
  159.0 2.4 %copy.56 = f32[8,4,2,6,1024]{4,2,3,1,0:T(2,128)} copy(f32[8,4,2,6,1024]{4,3,1,0,2:T(8,128)S(1)} %pad_maximum_fusion.2) | data formatting | bytes 3145728 | tf_op jit(solution)/shard_map/stack | solution.py:77
  (2 shorter events, 0.0 us)
Async XLA Ops:
  1.4 36.1 %all-to-all-start = ((s32[64,4,16]{2,1,0:T(4,128)}), s32[64,4,16]{2,1,0:T(4,128)S(1)}, u32[]{:S(2)}, u32[]{:S(2)}) async-start(s32[64,4,16]{2,1,0:T(4,128)} %broadcast_in_dim.5), calls=%async_computation | async-start | bytes 262144 | tf_op jit(solution)/shard_map/all_to_all | solution.py:19
  37.5 13.5 %copy-start.2 = (s32[3,512]{1,0:T(4,128)S(1)}, s32[3,512]{1,0:T(4,128)}, u32[]{:S(2)}) copy-start(s32[3,512]{1,0:T(4,128)} %param.8) | copy-start | bytes 18436
  37.5 67.0 %all-to-all-start.1 = ((bf16[256,16,1,2,96]{4,1,3,2,0:T(8,128)(2,1)}), bf16[256,16,1,2,96]{4,1,3,2,0:T(8,128)(2,1)S(1)}, u32[]{:S(2)}, u32[]{:S(2)}) async-start(bf16[256,16,1,2,96]{4,1,3,2,0:T(8,128)(2,1)} %copy.44), calls=%async_computation.1 | async-start | bytes 4194304 | tf_op jit(solution)/shard_map/all_to_all | solution.py:37
  104.5 1.3 copy-start
  114.4 6.4 %copy-start.1 = (f32[8,2,6,6]{0,1,3,2:T(2,128)S(1)}, f32[8,2,6,6]{0,1,3,2:T(2,128)}, u32[]{:S(2)}) copy-start(f32[8,2,6,6]{0,1,3,2:T(2,128)} %param.9) | copy-start | bytes 6916
  115.9 38.4 %all-to-all-start.2 = ((bf16[512,4,2,96]{3,1,2,0:T(4,128)(2,1)}), bf16[512,4,2,96]{3,1,2,0:T(4,128)(2,1)S(1)}, u32[]{:S(2)}, u32[]{:S(2)}) async-start(bf16[512,4,2,96]{3,1,2,0:T(4,128)(2,1)} %copy.49), calls=%async_computation.2 | async-start | bytes 2097152 | tf_op jit(solution)/shard_map/all_to_all | solution.py:81
where the time goes:
time: 162 us; the launch traced here: 161 us
  waiting for transfers between devices  72.9 us (45%)
  local copies, waits for them, and re-layouts  34.9 us (22%)
  starting transfers between devices  32.3 us (20%)
  other arithmetic  14.8 us (9%)
  matrix products  6.18 us (4%)
    all_to_all x1, waiting for transfers between devices, joined_exchange(): tiles = lax.all_to_all(tiles, axis, split_axis=0, concat_axis=0, tiled=True)  39.8 us
    all_to_all x1, waiting for transfers between devices, to_owners(): lax.all_to_all(all_points.astype(jnp.bfloat16), 'rp', split_axis=0, conca...  33.1 us
    all_to_all x1, starting transfers between devices, from_everyone(): lax.all_to_all(jnp.broadcast_to(x[None], (peers, *x.shape)), axis, 0, 0,...  13.9 us
    all_to_all x1, starting transfers between devices, joined_exchange(): tiles = lax.all_to_all(tiles, axis, split_axis=0, concat_axis=0, tiled=True)  13.5 us
    another operation x1, other arithmetic  11.5 us
    reshape x2, local copies, waits for them, and re-layouts, per_device(): coupling.reshape(local_rp, local_re, parts, mode_count, re_count, pair_sh...  6.25 us
    all_to_all x1, starting transfers between devices, to_owners(): lax.all_to_all(all_points.astype(jnp.bfloat16), 'rp', split_axis=0, conca...  4.92 us
    transpose x1, local copies, waits for them, and re-layouts, per_device(): reordered = jnp.swapaxes(reordered, 3, 4)  4.86 us
  transfers between devices with their start and end apart: 3, of which 2 were waited for; matrix products, arithmetic and copies ran while one was open for 22% of the time, Pallas kernels for 0%

commit v1 on v0

v1 whole, which is shorter than its diff:
```python
import functools
import math

import numpy as np

import jax
import jax.numpy as jnp
from jax import lax
from jax.experimental import pallas as pl
from jax.experimental.pallas import tpu as pltpu
from jax.sharding import PartitionSpec as P

MESH = pl.DeviceIdType.MESH
UNITS = 6
PEERS = 32
STEP = ((0, 0, 1, 2, 2, 3), (0, 1, 1, 2, 3, 3))
WHICH = ((0, 2, 0, 0, 2, 0), (1, 1, 2, 1, 1, 2))
PLANE = ((0, 1), (1, 0), (0, 3), (3, 0), (1, 1), (3, 3), (1, 3), (3, 1), (0, 2), (2, 0), (1, 2), (2, 1), (3, 2), (2, 3), (2, 2))
SINE = np.linalg.solve(
    np.array([[w ** (2 * i + 1) for i in range(4)] for w in (1.0, 2.0, 3.0, 4.0)]),
    np.sin(np.pi / 8 * np.arange(1, 5)),
)


def place():
    rp, lo = lax.axis_index("rp"), lax.axis_index("re")
    return rp // 16, (rp // 4) % 4, (rp // 2) % 2, rp % 2, lo


def pick(table, core, unit):
    if isinstance(core, int):
        return table[core][unit]
    return jnp.where(core == 0, table[0][unit], table[1][unit])


def exchange(lat, qt, coupling, out, held, x, lattice, table, y, g, f,
             load_sem, own_sem, lat_sem, x_send, x_recv, y_send, y_recv, f_send, f_recv):
    row, col, hi, core, lo = place()
    chip = row * 4 + col
    me = chip * 2 + core

    def plane_peer(d):
        r, c = (row + d[0]) % 4, (col + d[1]) % 4
        return r * 4 + c

    def peers():
        yield chip, 1 - core
        for d in PLANE:
            for c in (0, 1):
                yield plane_peer(d), c

    def plane_id(i, c):
        return ((i * 2 + hi) * 2 + c, lo)

    def z_id(z_hi, z_lo):
        return ((chip * 2 + z_hi) * 2 + core, z_lo)

    load = pltpu.make_async_copy(coupling, held, load_sem)
    load.start()
    barrier = pltpu.get_barrier_semaphore()
    for i, c in peers():
        pl.semaphore_signal(barrier, inc=1, device_id=plane_id(i, c), device_id_type=MESH)
    for d in range(1, 8):
        z = (hi * 4 + lo + d) % 8
        pl.semaphore_signal(barrier, inc=1, device_id=z_id(z // 4, z % 4), device_id_type=MESH)
    lattice[me] = lat[...]
    pl.semaphore_wait(barrier, PEERS - 1 + 7)

    for i, c in peers():
        pltpu.make_async_remote_copy(
            lat, lattice.at[me], lat_sem.at[0], lat_sem.at[1],
            device_id=plane_id(i, c), device_id_type=MESH,
        ).start()
    load.wait()

    def piece(ref, i, c, unit):
        p = (lo + pick(STEP, c, unit)) % 4
        mode = (i // 8) * 3 + pick(WHICH, c, unit)
        return ref.at[:, mode, p * 8 + i % 8]

    for unit in range(UNITS):
        pltpu.make_async_copy(piece(coupling, chip, core, unit), x.at[unit, me], own_sem.at[unit]).start()
        for i, c in peers():
            pltpu.make_async_remote_copy(
                piece(held, i, c, unit), x.at[unit, me], x_send.at[unit], x_recv.at[unit],
                device_id=plane_id(i, c), device_id_type=MESH,
            ).start()

    def wait(ref, sem):
        pltpu.make_async_copy(ref, ref, sem).wait()

    wait(lattice.at[pl.ds(0, PEERS - 1)], lat_sem.at[1])
    groups = []
    for n in range(PEERS // 4):
        quad = lattice[4 * n : 4 * n + 4].astype(jnp.float32)
        groups.append(quad[0] + quad[1] + quad[2] + quad[3])
    vectors = jnp.concatenate(groups, axis=1)
    weights = 1.0 / vectors[5:6]
    vectors = vectors.astype(jnp.bfloat16)
    rows = 256
    for n in range(1024 // rows):
        turns = jnp.dot(qt[n * rows : (n + 1) * rows, :], vectors, preferred_element_type=jnp.float32)
        turns = turns - 16.0 * jnp.floor(turns * (1.0 / 16.0))
        w = jnp.abs(turns - 8.0) - 4.0
        s = w * w
        value = w * (((float(SINE[3]) * s + float(SINE[2])) * s + float(SINE[1])) * s + float(SINE[0]))
        table[n * rows : (n + 1) * rows, :] = (value * weights).astype(jnp.bfloat16)

    def transform(unit):
        wait(x.at[unit, 0], own_sem.at[unit])
        wait(x.at[unit, pl.ds(0, PEERS - 1)], x_recv.at[unit])
        part = jnp.dot(
            table[...], x.at[unit].reshape(1024, 128)[...], preferred_element_type=jnp.float32
        )
        y[unit] = part.astype(jnp.bfloat16).reshape(2, 512, 128)
        p = (lo + pick(STEP, core, unit)) % 4

        def send(z_hi):
            pltpu.make_async_remote_copy(
                y.at[unit, z_hi], g.at[unit, hi], y_send.at[unit, z_hi], y_recv.at[unit, hi],
                device_id=z_id(z_hi, p), device_id_type=MESH,
            ).start()

        def keep():
            g[unit, hi] = y[unit, hi]

        send(1 - hi)
        if unit == 0:
            keep()
        elif unit == 1:
            pl.when(core == 0)(keep)
            pl.when(core == 1)(lambda: send(hi))
        else:
            send(hi)

    def spread(unit):
        wait(g.at[unit, 1 - hi], y_recv.at[unit, 1 - hi])
        if unit == 1:
            pl.when(core == 1)(lambda: wait(g.at[unit, hi], y_recv.at[unit, hi]))
        elif unit > 1:
            wait(g.at[unit, hi], y_recv.at[unit, hi])
        total = g[unit, 0].astype(jnp.float32) + g[unit, 1].astype(jnp.float32)
        f.at[unit].reshape(512, 128)[...] = total.astype(jnp.bfloat16)
        re = (lo + 4 - pick(STEP, core, unit)) % 4
        mode = (chip // 8) * 3 + pick(WHICH, core, unit)
        place_of = out.at[:, re, mode, chip % 8]
        for i, c in peers():
            pltpu.make_async_remote_copy(
                f.at[unit, i * 2 + c], place_of, f_send.at[unit], f_recv.at[unit],
                device_id=plane_id(i, c), device_id_type=MESH,
            ).start()
        place_of[...] = f[unit, me]

    lag = 2
    for unit in range(UNITS):
        transform(unit)
        if unit >= lag:
            spread(unit - lag)
    for unit in range(UNITS - lag, UNITS):
        spread(unit)
    for unit in range(UNITS):
        wait(f.at[unit, pl.ds(0, PEERS - 1)], f_recv.at[unit])
    wait(lattice.at[pl.ds(0, PEERS - 1)], lat_sem.at[0])
    for unit in range(UNITS):
        wait(x.at[unit, pl.ds(0, PEERS - 1)], x_send.at[unit])
        wait(f.at[unit, pl.ds(0, PEERS - 1)], f_send.at[unit])
        wait(y.at[unit, 1 - hi], y_send.at[unit, 1 - hi])
        if unit == 1:
            pl.when(core == 1)(lambda: wait(y.at[unit, hi], y_send.at[unit, hi]))
        elif unit > 1:
            wait(y.at[unit, hi], y_send.at[unit, hi])


def rotate(vec, summed, out):
    q = pl.program_id(0)
    odd = lax.broadcasted_iota(jnp.int32, (16, 128), 0) % 2 == 1
    flat = summed.reshape(1, 4, 6, 16, 128)
    flat_out = out.reshape(1, 4, 6, 16, 128)
    for re in range(4):
        plain = [flat[0, re, k].astype(jnp.float32) for k in range(6)]
        turned = [jnp.where(odd, pltpu.roll(v, 1, 0), -pltpu.roll(v, 15, 0)) for v in plain]
        for n in range(6):
            total = None
            for k in range(6):
                term = vec[q, 0, k, n] * plain[k] + vec[q, 1, k, n] * turned[k]
                total = term if total is None else total + term
            flat_out[0, re, n] = total


def per_device(coupling, rp_coords, degeneracy, qpoints, eigvec):
    me = (lax.axis_index("rp") // 4) * 2 + lax.axis_index("rp") % 2
    lane = jnp.arange(128)
    ones = jnp.ones((1, 16), jnp.int32)
    stacked = jnp.concatenate([rp_coords, 0 * ones, ones, degeneracy[None], 0 * ones, 0 * ones], axis=0)
    lat = jnp.tile(jnp.repeat(stacked, 2, axis=1), (1, 4))
    lat = lat + jnp.where((jnp.arange(8) == 3)[:, None], 4 * (lane % 2)[None], 0)
    lat = jnp.where((lane // 32 == me % 4)[None], lat, 0).astype(jnp.bfloat16)
    points = qpoints.reshape(3, 16, 2, 2, 8).transpose(0, 2, 1, 3, 4).reshape(3, 512)
    points = jnp.repeat(points, 2, axis=1)
    unit_row = jnp.ones((1, 1024), jnp.int32)
    half = (-4 * (jnp.arange(1024) % 2))[None].astype(jnp.int32)
    qt = jnp.concatenate([points, unit_row, half, 0 * points], axis=0).T.astype(jnp.bfloat16)
    blocks = coupling.reshape(16, 2, 6, 32, 128).transpose(0, 2, 3, 1, 4)
    vmem = pl.BlockSpec(memory_space=pltpu.VMEM)
    dma = pltpu.SemaphoreType.DMA
    bf = jnp.bfloat16
    summed = pl.pallas_call(
        exchange,
        out_shape=jax.ShapeDtypeStruct((8, 4, 6, 8, 2, 128), bf),
        in_specs=[vmem, vmem, pl.BlockSpec(memory_space=pl.ANY)],
        out_specs=vmem,
        scratch_shapes=[
            pltpu.VMEM((16, 6, 32, 2, 128), bf),
            pltpu.VMEM((UNITS, PEERS, 16, 2, 128), bf),
            pltpu.VMEM((PEERS, 8, 128), bf),
            pltpu.VMEM((1024, 1024), bf),
            pltpu.VMEM((UNITS, 2, 512, 128), bf),
            pltpu.VMEM((UNITS, 2, 512, 128), bf),
            pltpu.VMEM((UNITS, PEERS, 8, 2, 128), bf),
            dma, dma((UNITS,)), dma((2,)), dma((UNITS,)), dma((UNITS,)),
            dma((UNITS, 2)), dma((UNITS, 2)), dma((UNITS,)), dma((UNITS,)),
        ],
        compiler_params=pltpu.CompilerParams(
            collective_id=0, has_side_effects=True, vmem_limit_bytes=40 * 2**20
        ),
        name="exchange",
    )(lat, qt, blocks)
    block = (1, 4, 6, 8, 2, 128)
    spec = pl.BlockSpec(block, lambda q: (q, 0, 0, 0, 0, 0))
    mixed = pl.pallas_call(
        rotate,
        grid=(8,),
        out_shape=jax.ShapeDtypeStruct((8, 4, 6, 8, 2, 128), jnp.float32),
        in_specs=[pl.BlockSpec(memory_space=pltpu.SMEM), spec],
        out_specs=spec,
        name="rotate",
    )(eigvec, summed)
    return mixed.transpose(0, 1, 4, 2, 3, 5).reshape(8, 4, 2, 6, 1024)


def solution(mesh):
    return jax.shard_map(
        per_device,
        mesh=mesh,
        in_specs=(
            P("rp", "re", None, None, None),
            P(None, "rp"),
            P("rp"),
            P(),
            P("rp", None, None, None),
        ),
        out_specs=P("rp", None, None, None, "re"),
        check_vma=False,
    )
```

time: 162 us -> 78.9 us (0.49)
  the two profiles are of different devices: /device:TPU:33 before, /device:TPU:1 now
where the time goes in v1:
time: 78.9 us; the launch traced here: 78.4 us
  Pallas kernels  72.6 us (92%)
  local copies, waits for them, and re-layouts  4.82 us (6%)
  other arithmetic  0.88 us (1%)
    pallas_call x1, Pallas kernels, per_device(): pl.pallas_call(exchange, out_shape=jax.ShapeDtypeStruct((8, 4, 6, 8, 2, 1...  62.6 us
    pallas_call x1, Pallas kernels, per_device(): pl.pallas_call(rotate, grid=(8,), out_shape=jax.ShapeDtypeStruct((8, 4, 6...  9.96 us
    unnamed x5, local copies, waits for them, and re-layouts  2.4 us

profile of v1, /device:TPU:1, one launch (start us, length us, event | category | flops | bytes accessed | tf_op | source)
XLA Modules:
  0.0 78.4 jit_solution(8877530363695577910)
XLA Ops:
  0.0 0.0 copy-start.1
  0.0 0.1 pad.1.clone
  0.1 0.1 pad.3.clone
  0.2 0.8 %concatenate.11 = s32[8,16]{1,0:T(8,128)S(1)} concatenate(s32[3,16]{1,0:T(4,128)} %param.6, s32[1,16]{1,0:T(1,128)S(1)} %broadcast.125, s32[1,16]{1,0:T(1,128)S(1)} %broadcast.126, s32[1,16]{1,0:T(1,128)} %bitcast.15, s32[2,16]{1,0:T(2,128)S(1)} %concatenate.10), dimensions={0} | concatenate | bytes 1024 | tf_op jit(solution)/shard_map/concatenate | solution.py:194
  1.0 0.1 copy.17
  1.1 0.7 convert.16
  1.8 0.1 copy.18
  1.9 0.1 tile.12
  2.0 0.1 select_convert_fusion.lat
  2.0 0.1 reshape.80
  2.2 0.1 reshape.79
  2.3 1.5 %copy.21.vec = f32[8,2,6,6]{3,2,1,0:T(8,128)} copy(f32[8,2,6,6]{0,1,3,2:T(2,128)} %param.9) | data formatting | bytes 4608 | tf_op args[4]
  3.9 0.3 broadcast_in_dim.54
  4.1 0.5 reshape.76
  4.6 0.1 maximum_maximum_fusion
  4.7 0.2 copy.20
  4.9 0.0 copy-done.1
  4.9 62.6 %exchange.1.summed = bf16[8,4,6,8,2,128]{5,4,3,2,1,0:T(2,128)(2,1)S(1)} custom-call(bf16[8,128]{1,0:T(8,128)(2,1)S(1)} %select_convert_fusion.lat, bf16[1024,8]{1,0:T(8,128)(2,1)S(1)} %bitcast.12, bf16[16,6,32,2,128]{4,3,2,1,0:T(2,128)(2,1)S(1)} %bitcast.11), custom_call_target="tpu_custom_call" | custom-call | tf_op jit(solution)/shard_map/exchange/pallas_call | solution.py:207
  67.5 0.0 copy-start
  67.5 0.9 %copy-done = bf16[8,4,6,8,2,128]{5,4,3,2,1,0:T(2,128)(2,1)} copy-done((bf16[8,4,6,8,2,128]{5,4,3,2,1,0:T(2,128)(2,1)}, bf16[8,4,6,8,2,128]{5,4,3,2,1,0:T(2,128)(2,1)S(1)}, u32[]{:S(2)}) %copy-start) | copy-done | bytes 786456
  68.4 10.0 %rotate.1 = f32[8,4,6,8,2,128]{5,4,3,2,1,0:T(2,128)} custom-call(f32[8,2,6,6]{3,2,1,0:T(8,128)} %copy.21.vec, bf16[8,4,6,8,2,128]{5,4,3,2,1,0:T(2,128)(2,1)} %copy-done), custom_call_target="tpu_custom_call" | custom-call | tf_op jit(solution)/shard_map/rotate/pallas_call | solution.py:230
  (11 shorter events, 0.1 us)
Async XLA Ops:
  0.0 4.9 %copy-start.1 = (bf16[16,1,2,6,4096]{4,2,3,1,0:T(2,128)(2,1)S(1)}, bf16[16,1,2,6,4096]{4,2,3,1,0:T(2,128)(2,1)}, u32[]{:S(2)}) copy-start(bf16[16,1,2,6,4096]{4,2,3,1,0:T(2,128)(2,1)} %param.5) | copy-start | bytes 4718596
  67.5 0.9 %copy-start = (bf16[8,4,6,8,2,128]{5,4,3,2,1,0:T(2,128)(2,1)}, bf16[8,4,6,8,2,128]{5,4,3,2,1,0:T(2,128)(2,1)S(1)}, u32[]{:S(2)}) copy-start(bf16[8,4,6,8,2,128]{5,4,3,2,1,0:T(2,128)(2,1)S(1)} %exchange.1.summed) | copy-start | bytes 2359300

commit v2 on v1

v2 whole, which is shorter than its diff:
```python
import functools
import math

import numpy as np

import jax
import jax.numpy as jnp
from jax import lax
from jax.experimental import pallas as pl
from jax.experimental.pallas import tpu as pltpu
from jax.sharding import PartitionSpec as P

MESH = pl.DeviceIdType.MESH
UNITS = 6
PEERS = 32
STEP = ((0, 0, 1, 3, 2, 2), (0, 3, 3, 1, 1, 2))
WHICH = ((0, 2, 0, 0, 0, 2), (1, 1, 2, 1, 2, 1))
PLANE = ((2, 2), (2, 1), (1, 2), (2, 3), (3, 2), (1, 1), (3, 3), (1, 3), (3, 1), (2, 0), (0, 2), (0, 1), (1, 0), (0, 3), (3, 0))
SINE = np.linalg.solve(
    np.array([[w ** (2 * i + 1) for i in range(4)] for w in (1.0, 2.0, 3.0, 4.0)]),
    np.sin(np.pi / 8 * np.arange(1, 5)),
)


def place():
    rp, lo = lax.axis_index("rp"), lax.axis_index("re")
    return rp // 16, (rp // 4) % 4, (rp // 2) % 2, rp % 2, lo


def pick(table, core, unit):
    if isinstance(core, int):
        return table[core][unit]
    return jnp.where(core == 0, table[0][unit], table[1][unit])


def exchange(coords_in, degeneracy_in, points_in, eigvec_in, coupling, out, coords, degeneracy, points, eigvec, held, x, own, lattice, table, y, g, f, summed, coef, doubled,
             load_sem, small_sem, lat_sem, x_send, x_recv, y_send, y_recv, f_send, f_recv):
    row, col, hi, core, lo = place()
    chip = row * 4 + col
    me = chip * 2 + core
    f32, bf16 = jnp.float32, jnp.bfloat16

    def plane_peer(d):
        r, c = (row + d[0]) % 4, (col + d[1]) % 4
        return r * 4 + c

    def peers():
        for c in (0, 1):
            for d in PLANE:
                yield plane_peer(d), c
        yield chip, 1 - core

    def plane_id(i, c):
        return ((i * 2 + hi) * 2 + c, lo)

    def z_id(z_hi, z_lo):
        return ((chip * 2 + z_hi) * 2 + core, z_lo)

    def iota(shape, dim):
        return lax.broadcasted_iota(jnp.int32, shape, dim)

    load = pltpu.make_async_copy(coupling, held, load_sem)
    small = [
        pltpu.make_async_copy(src, dst, small_sem.at[n])
        for n, (src, dst) in enumerate(
            ((coords_in, coords), (degeneracy_in, degeneracy), (points_in, points), (eigvec_in, eigvec))
        )
    ]
    for copy in small:
        copy.start()
    load.start()
    barrier = pltpu.get_barrier_semaphore()
    for i, c in peers():
        pl.semaphore_signal(barrier, inc=1, device_id=plane_id(i, c), device_id_type=MESH)
    for d in range(1, 8):
        z = (hi * 4 + lo + d) % 8
        pl.semaphore_signal(barrier, inc=1, device_id=z_id(z // 4, z % 4), device_id_type=MESH)

    for copy in small:
        copy.wait()
    zeros = functools.partial(jnp.zeros, dtype=f32)
    stacked = jnp.concatenate(
        [coords[...].astype(f32), zeros((2, 16)), degeneracy[...].astype(f32), zeros((2, 16))], axis=0
    )
    spread16 = (iota((16, 128), 0) == iota((16, 128), 1) % 32 // 2).astype(f32)
    lat = jnp.dot(stacked, spread16, preferred_element_type=f32)
    line, lane = iota((8, 128), 0), iota((8, 128), 1)
    lat = lat + jnp.where(line == 3, 4 * (lane % 2), jnp.where(line == 4, 1, 0)).astype(f32)
    own[...] = jnp.where(lane // 32 == me % 4, lat, 0.0).astype(bf16)
    lattice[me] = own[...]
    grid = jnp.concatenate([points[...].astype(f32), zeros((5, 512))], axis=0)
    twice = []
    lane = iota((128, 256), 1)
    pair = (iota((128, 256), 0) == lane % 128 // 32 * 32 + lane // 128 * 16 + lane % 32 // 2).astype(f32)
    for n in range(4):
        twice.append(jnp.dot(grid[:, 128 * n : 128 * n + 128], pair, preferred_element_type=f32))
    line, lane = iota((8, 512), 0), iota((8, 512), 1)
    extra = jnp.where(line == 3, 1, jnp.where(line == 4, -4 * (lane % 2), 0)).astype(f32)
    for h in range(2):
        doubled[h] = jnp.concatenate([t[:, 128 * h : 128 * h + 128] for t in twice], axis=1) + extra
    rows16 = (iota((16, 8), 0) // 2 == iota((16, 8), 1)).astype(f32)
    columns = lax.dot_general(
        rows16, eigvec[...], (((1,), (1,)), ((), ())), precision=lax.Precision.HIGHEST, preferred_element_type=f32
    )
    for n in range(72):
        coef[n] = jnp.broadcast_to(columns[:, n : n + 1], (16, 128))

    pl.semaphore_wait(barrier, PEERS - 1 + 7)

    for i, c in peers():
        pltpu.make_async_remote_copy(
            own, lattice.at[me], lat_sem.at[0], lat_sem.at[1],
            device_id=plane_id(i, c), device_id_type=MESH,
        ).start()
    load.wait()

    def piece(ref, i, c, unit):
        p = (lo + pick(STEP, c, unit)) % 4
        mode = (i // 8) * 3 + pick(WHICH, c, unit)
        return ref.at[:, mode, p * 8 + i % 8]

    for unit in range(UNITS):
        for i, c in peers():
            pltpu.make_async_remote_copy(
                piece(held, i, c, unit), x.at[unit, me], x_send.at[unit], x_recv.at[unit],
                device_id=plane_id(i, c), device_id_type=MESH,
            ).start()
    for unit in range(UNITS):
        x[unit, me] = piece(held, chip, core, unit)[...]

    def wait(ref, sem):
        pltpu.make_async_copy(ref, ref, sem).wait()

    wait(lattice.at[pl.ds(0, PEERS - 1)], lat_sem.at[1])
    groups = []
    for n in range(PEERS // 4):
        quad = lattice[4 * n : 4 * n + 4].astype(f32)
        groups.append(quad[0] + quad[1] + quad[2] + quad[3])
    vectors = jnp.concatenate(groups, axis=1)
    weights = 1.0 / vectors[5:6]
    def tabulate(half):
        for n in range(2):
            turns = lax.dot_general(
                doubled.at[half][:, n * 256 : (n + 1) * 256], vectors,
                (((0,), (0,)), ((), ())), preferred_element_type=f32,
            )
            turns = turns - 16.0 * jnp.floor(turns * (1.0 / 16.0))
            w = jnp.abs(turns - 8.0) - 4.0
            s = w * w
            value = w * (((float(SINE[3]) * s + float(SINE[2])) * s + float(SINE[1])) * s + float(SINE[0]))
            table.at[half][n * 256 : (n + 1) * 256, :] = (value * weights).astype(bf16)

    def send(unit, half):
        p = (lo + pick(STEP, core, unit)) % 4
        pltpu.make_async_remote_copy(
            y.at[unit, half], g.at[unit, hi], y_send.at[unit, half], y_recv.at[unit, hi],
            device_id=z_id(half, p), device_id_type=MESH,
        ).start()

    def contract(unit, half, target):
        part = jnp.dot(table[half], x.at[unit].reshape(1024, 128)[...], preferred_element_type=f32)
        target[...] = part.astype(bf16)

    def transform(unit):
        wait(x.at[unit, pl.ds(0, PEERS - 1)], x_recv.at[unit])
        contract(unit, 1 - hi, y.at[unit, 1 - hi])
        send(unit, 1 - hi)
        if unit == 0:
            tabulate(hi)
            contract(unit, hi, g.at[unit, hi])
        elif unit == 1:
            contract(unit, hi, y.at[unit, hi])

            @pl.when(core == 0)
            def keep():
                g[unit, hi] = y[unit, hi]

            pl.when(core == 1)(lambda: send(unit, hi))
        else:
            contract(unit, hi, y.at[unit, hi])
            send(unit, hi)

    tabulate(1 - hi)

    def spread(unit):
        wait(g.at[unit, 1 - hi], y_recv.at[unit, 1 - hi])
        if unit == 1:
            pl.when(core == 1)(lambda: wait(g.at[unit, hi], y_recv.at[unit, hi]))
        elif unit > 1:
            wait(g.at[unit, hi], y_recv.at[unit, hi])
        total = g[unit, 0].astype(f32) + g[unit, 1].astype(f32)
        f[unit * PEERS : (unit + 1) * PEERS] = total.astype(bf16).reshape(PEERS, 16, 128)
        step = pick(STEP, core, unit)
        mode = (chip // 8) * 3 + pick(WHICH, core, unit)
        place_of = summed.at[step, mode, chip % 8]
        for i, c in peers():
            pltpu.make_async_remote_copy(
                f.at[unit * PEERS + i * 2 + c], place_of, f_send.at[unit], f_recv.at[step],
                device_id=plane_id(i, c), device_id_type=MESH,
            ).start()
        place_of[...] = f[unit * PEERS + me]

    odd = iota((16, 128), 0) % 2 == 1

    def rotate(step):
        for c in (0, 1):
            mine = 2 if c == step % 2 else 1
            pl.when(core == c)(lambda: wait(f.at[pl.ds(0, 48 - mine)], f_recv.at[step]))
        re = (lo + 4 - step) % 4

        def block(b, _):
            plain = [summed[step, k, b].astype(f32) for k in range(6)]
            turned = [jnp.where(odd, pltpu.roll(v, 1, 0), -pltpu.roll(v, 15, 0)) for v in plain]
            for n in range(6):
                total = None
                for k in range(6):
                    at = (k * 6 + n) * 2
                    term = coef[at] * plain[k] + coef[at + 1] * turned[k]
                    total = term if total is None else total + term
                out[:, re, n, b] = total.reshape(8, 2, 128)
            return 0

        lax.fori_loop(0, 8, block, 0)

    lag = 4
    for unit in range(UNITS):
        transform(unit)
        if unit >= lag:
            spread(unit - lag)
    for unit in range(UNITS - lag, UNITS):
        spread(unit)
    wait(lattice.at[pl.ds(0, PEERS - 1)], lat_sem.at[0])
    for unit in range(UNITS):
        wait(x.at[unit, pl.ds(0, PEERS - 1)], x_send.at[unit])
        wait(g.at[unit, 0], y_send.at[unit, 1 - hi])
        if unit == 1:
            pl.when(core == 1)(lambda: wait(g.at[unit, 0], y_send.at[unit, hi]))
        elif unit > 1:
            wait(g.at[unit, 0], y_send.at[unit, hi])
    for step in (0, 3, 1, 2):
        rotate(step)
    for unit in range(UNITS):
        wait(f.at[pl.ds(0, PEERS - 1)], f_send.at[unit])


def per_device(coupling, rp_coords, degeneracy, qpoints, eigvec):
    blocks = coupling.reshape(16, 2, 6, 32, 128).transpose(0, 2, 3, 1, 4)
    vectors = eigvec.transpose(2, 3, 1, 0).reshape(72, 8)
    vmem = pl.BlockSpec(memory_space=pltpu.VMEM)
    dma = pltpu.SemaphoreType.DMA
    bf = jnp.bfloat16
    mixed = pl.pallas_call(
        exchange,
        out_shape=jax.ShapeDtypeStruct((8, 4, 6, 8, 2, 128), jnp.float32),
        in_specs=[pl.BlockSpec(memory_space=pl.ANY)] * 5,
        out_specs=vmem,
        scratch_shapes=[
            pltpu.VMEM((3, 16), jnp.int32),
            pltpu.VMEM((1, 16), jnp.int32),
            pltpu.VMEM((3, 512), jnp.int32),
            pltpu.VMEM((72, 8), jnp.float32),
            pltpu.VMEM((16, 6, 32, 2, 128), bf),
            pltpu.VMEM((UNITS, PEERS, 16, 2, 128), bf),
            pltpu.VMEM((8, 128), bf),
            pltpu.VMEM((PEERS, 8, 128), bf),
            pltpu.VMEM((2, 512, 1024), bf),
            pltpu.VMEM((UNITS, 2, 512, 128), bf),
            pltpu.VMEM((UNITS, 2, 512, 128), bf),
            pltpu.VMEM((UNITS * PEERS, 16, 128), bf),
            pltpu.VMEM((4, 6, 8, 16, 128), bf),
            pltpu.VMEM((72, 16, 128), jnp.float32),
            pltpu.VMEM((2, 8, 512), jnp.float32),
            dma, dma((4,)), dma((2,)), dma((UNITS,)), dma((UNITS,)),
            dma((UNITS, 2)), dma((UNITS, 2)), dma((UNITS,)), dma((4,)),
        ],
        compiler_params=pltpu.CompilerParams(
            collective_id=0, has_side_effects=True, vmem_limit_bytes=40 * 2**20
        ),
        name="exchange",
    )(*(pltpu.with_memory_space_constraint(v, pltpu.HBM) for v in (rp_coords, degeneracy.reshape(1, 16), qpoints, vectors, blocks)))
    return mixed.transpose(0, 1, 4, 2, 3, 5).reshape(8, 4, 2, 6, 1024)


def solution(mesh):
    return jax.shard_map(
        per_device,
        mesh=mesh,
        in_specs=(
            P("rp", "re", None, None, None),
            P(None, "rp"),
            P("rp"),
            P(),
            P("rp", None, None, None),
        ),
        out_specs=P("rp", None, None, None, "re"),
        check_vma=False,
    )
```

time: 78.9 us -> 60.8 us (0.77)
  Pallas kernels: 72.6 us -> 59.6 us
  local copies, waits for them, and re-layouts: 4.82 us -> 1.15 us
  other arithmetic: 0.88 us -> 0 us
    pallas_call x1 -> x0, Pallas kernels: 9.96 us -> none  [per_device(): pl.pallas_call(rotate, grid=(8,), out_shape=jax.ShapeDtypeStruct((8, 4, 6...]
    pallas_call x1, Pallas kernels: 62.6 us -> 59.6 us  [per_device(): pl.pallas_call(exchange, out_shape=jax.ShapeDtypeStruct((8, 4, 6, 8, 2, 1...]
    unnamed x5 -> x1, local copies, waits for them, and re-layouts: 2.4 us -> 1.15 us
    concatenate x6 -> x0, local copies, waits for them, and re-layouts: 1.21 us -> none  [the longest x3 0.88 us: per_device(): jnp.concatenate([rp_coords, 0 * ones, ones, degeneracy[None], 0 * ones, 0...]
where the time goes in v2:
time: 60.8 us; the launch traced here: 60.7 us
  Pallas kernels  59.6 us (98%)
  local copies, waits for them, and re-layouts  1.15 us (2%)
    pallas_call x1, Pallas kernels, per_device(): pl.pallas_call(exchange, out_shape=jax.ShapeDtypeStruct((8, 4, 6, 8, 2, 1...  59.6 us

profile of v2, /device:TPU:1, one launch (start us, length us, event | category | flops | bytes accessed | tf_op | source)
XLA Modules:
  0.0 60.7 jit_solution(7931278525908892774)
XLA Ops:
  0.0 59.6 %exchange.1 = f32[8,4,6,8,2,128]{5,4,3,2,1,0:T(2,128)S(1)} custom-call(s32[3,16]{1,0:T(4,128)} %coords_in.1, s32[1,16]{1,0:T(1,128)} %bitcast.13, s32[3,512]{1,0:T(4,128)} %points_in.1, f32[72,8]{1,0:T(8,128)} %bitcast.12, bf16[16,6,32,2,128]{4,3,2,1,0:T(2,128)(2,1)} %bitcast.11), custom_call_target="tpu_custom_call" | custom-call | tf_op jit(solution)/shard_map/exchange/pallas_call | solution.py:252
  59.6 1.1 %copy.7 = f32[8,4,2,6,1024]{4,2,3,1,0:T(2,128)} copy(f32[8,4,2,6,1024]{4,2,3,1,0:T(2,128)S(1)} %bitcast.10) | data formatting | bytes 3145728

commit v3 on v2

--- a/solution.py
+++ b/solution.py
@@ -13,8 +13,11 @@
 MESH = pl.DeviceIdType.MESH
 UNITS = 6
 PEERS = 32
-STEP = ((0, 0, 1, 3, 2, 2), (0, 3, 3, 1, 1, 2))
-WHICH = ((0, 2, 0, 0, 0, 2), (1, 1, 2, 1, 2, 1))
+LATE = (3, 4, 5)
+JOINT = 5
+EARLY = 3
+STEP = ((0, 0, 2, 3, 1, 2), (0, 3, 1, 3, 1, 2))
+WHICH = ((0, 2, 0, 0, 0, 2), (1, 2, 2, 1, 1, 1))
 PLANE = ((2, 2), (2, 1), (1, 2), (2, 3), (3, 2), (1, 1), (3, 3), (1, 3), (3, 1), (2, 0), (0, 2), (0, 1), (1, 0), (0, 3), (3, 0))
 SINE = np.linalg.solve(
     np.array([[w ** (2 * i + 1) for i in range(4)] for w in (1.0, 2.0, 3.0, 4.0)]),
@@ -33,8 +36,8 @@
     return jnp.where(core == 0, table[0][unit], table[1][unit])
 
 
-def exchange(coords_in, degeneracy_in, points_in, eigvec_in, coupling, out, coords, degeneracy, points, eigvec, held, x, own, lattice, table, y, g, f, summed, coef, doubled,
-             load_sem, small_sem, lat_sem, x_send, x_recv, y_send, y_recv, f_send, f_recv):
+def exchange(coords_in, degeneracy_in, points_in, eigvec_in, coupling, out, coords, degeneracy, points, eigvec, held, x, own, lattice, table, y, g, f, summed, coef, doubled, relayed, joined, partner, others, raw, joint_relayed, joint_g,
+             load_sem, small_sem, lat_sem, relay_sem, side_sem, joint_send, joint_recv, x_send, x_recv, y_send, y_recv, f_send, f_recv):
     row, col, hi, core, lo = place()
     chip = row * 4 + col
     me = chip * 2 + core
@@ -76,6 +79,7 @@
         z = (hi * 4 + lo + d) % 8
         pl.semaphore_signal(barrier, inc=1, device_id=z_id(z // 4, z % 4), device_id_type=MESH)
 
+    pl.semaphore_wait(barrier, PEERS - 1 + 7)
     for copy in small:
         copy.wait()
     zeros = functools.partial(jnp.zeros, dtype=f32)
@@ -88,6 +92,59 @@
     lat = lat + jnp.where(line == 3, 4 * (lane % 2), jnp.where(line == 4, 1, 0)).astype(f32)
     own[...] = jnp.where(lane // 32 == me % 4, lat, 0.0).astype(bf16)
     lattice[me] = own[...]
+
+    for i, c in peers():
+        pltpu.make_async_remote_copy(
+            own, lattice.at[me], lat_sem.at[0], lat_sem.at[1],
+            device_id=plane_id(i, c), device_id_type=MESH,
+        ).start()
+    pltpu.make_async_remote_copy(
+        own, partner, side_sem.at[0], side_sem.at[1], device_id=z_id(1 - hi, lo), device_id_type=MESH
+    ).start()
+    load.wait()
+    joint_p = (lo + STEP[0][JOINT]) % 4
+    for n in range(2):
+        pltpu.make_async_remote_copy(
+            held.at[:, 3 * n + pick(WHICH, 1 - hi, JOINT), pl.ds(joint_p * 8, 8)], raw.at[n],
+            side_sem.at[2], side_sem.at[3], device_id=z_id(1 - hi, lo), device_id_type=MESH,
+        ).start()
+
+    def piece(ref, i, c, unit):
+        p = (lo + pick(STEP, c, unit)) % 4
+        mode = (i // 8) * 3 + pick(WHICH, c, unit)
+        return ref.at[:, mode, p * 8 + i % 8]
+
+    def scatter(unit):
+        for i, c in peers():
+            pltpu.make_async_remote_copy(
+                piece(held, i, c, unit), x.at[unit, me], x_send.at[unit], x_recv.at[unit],
+                device_id=plane_id(i, c), device_id_type=MESH,
+            ).start()
+
+    for unit in range(EARLY):
+        scatter(unit)
+
+    def hand_on(source, n):
+        def to(i):
+            pltpu.make_async_remote_copy(
+                source(i), joined.at[n, me], joint_send.at[n], joint_recv.at[n],
+                device_id=plane_id(i, hi), device_id_type=MESH,
+            ).start()
+
+        for d in PLANE:
+            to(plane_peer(d))
+        pl.when(core != hi)(lambda: to(chip))
+
+        @pl.when(core == hi)
+        def keep():
+            joined[n, me] = source(chip)[...]
+
+    for unit in range(JOINT):
+        x[unit, me] = piece(held, chip, core, unit)[...]
+
+    def wait(ref, sem):
+        pltpu.make_async_copy(ref, ref, sem).wait()
+
     grid = jnp.concatenate([points[...].astype(f32), zeros((5, 512))], axis=0)
     twice = []
     lane = iota((128, 256), 1)
@@ -105,40 +162,17 @@
     for n in range(72):
         coef[n] = jnp.broadcast_to(columns[:, n : n + 1], (16, 128))
 
-    pl.semaphore_wait(barrier, PEERS - 1 + 7)
-
-    for i, c in peers():
-        pltpu.make_async_remote_copy(
-            own, lattice.at[me], lat_sem.at[0], lat_sem.at[1],
-            device_id=plane_id(i, c), device_id_type=MESH,
-        ).start()
-    load.wait()
-
-    def piece(ref, i, c, unit):
-        p = (lo + pick(STEP, c, unit)) % 4
-        mode = (i // 8) * 3 + pick(WHICH, c, unit)
-        return ref.at[:, mode, p * 8 + i % 8]
-
-    for unit in range(UNITS):
-        for i, c in peers():
-            pltpu.make_async_remote_copy(
-                piece(held, i, c, unit), x.at[unit, me], x_send.at[unit], x_recv.at[unit],
-                device_id=plane_id(i, c), device_id_type=MESH,
-            ).start()
-    for unit in range(UNITS):
-        x[unit, me] = piece(held, chip, core, unit)[...]
-
-    def wait(ref, sem):
-        pltpu.make_async_copy(ref, ref, sem).wait()
-
     wait(lattice.at[pl.ds(0, PEERS - 1)], lat_sem.at[1])
-    groups = []
-    for n in range(PEERS // 4):
-        quad = lattice[4 * n : 4 * n + 4].astype(f32)
-        groups.append(quad[0] + quad[1] + quad[2] + quad[3])
-    vectors = jnp.concatenate(groups, axis=1)
-    weights = 1.0 / vectors[5:6]
-    def tabulate(half):
+    def gathered(ref):
+        groups = []
+        for n in range(PEERS // 4):
+            quad = ref[4 * n : 4 * n + 4].astype(f32)
+            groups.append(quad[0] + quad[1] + quad[2] + quad[3])
+        return jnp.concatenate(groups, axis=1)
+
+    def tabulate(vectors, which, half):
+        weights = 1.0 / vectors[5:6]
+        vectors = vectors.astype(bf16)
         for n in range(2):
             turns = lax.dot_general(
                 doubled.at[half][:, n * 256 : (n + 1) * 256], vectors,
@@ -148,7 +182,7 @@
             w = jnp.abs(turns - 8.0) - 4.0
             s = w * w
             value = w * (((float(SINE[3]) * s + float(SINE[2])) * s + float(SINE[1])) * s + float(SINE[0]))
-            table.at[half][n * 256 : (n + 1) * 256, :] = (value * weights).astype(bf16)
+            table.at[which, half][n * 256 : (n + 1) * 256, :] = (value * weights).astype(bf16)
 
     def send(unit, half):
         p = (lo + pick(STEP, core, unit)) % 4
@@ -158,15 +192,30 @@
         ).start()
 
     def contract(unit, half, target):
-        part = jnp.dot(table[half], x.at[unit].reshape(1024, 128)[...], preferred_element_type=f32)
-        target[...] = part.astype(bf16)
+        part = jnp.dot(table[0, half], x.at[unit].reshape(1024, 128)[...], preferred_element_type=f32)
+        target[...] = part.astype(bf16).reshape(PEERS, 16, 128)
 
     def transform(unit):
         wait(x.at[unit, pl.ds(0, PEERS - 1)], x_recv.at[unit])
+        if unit in LATE:
+            n = LATE.index(unit)
+            for half in (0, 1):
+                contract(unit, half, y.at[unit, half])
+            for i, c in peers():
+                pltpu.make_async_remote_copy(
+                    y.at[unit, :, i * 2 + c], relayed.at[n, :, me], relay_sem.at[0, n], relay_sem.at[1, n],
+                    device_id=plane_id(i, c), device_id_type=MESH,
+                ).start()
+            relayed[n, :, me] = y[unit, :, me]
+            return
         contract(unit, 1 - hi, y.at[unit, 1 - hi])
         send(unit, 1 - hi)
         if unit == 0:
-            tabulate(hi)
+            forward_lattice()
+            for later in range(EARLY, JOINT):
+                scatter(later)
+            hand_on(lambda i: piece(held, i, hi, JOINT), 0)
+            tabulate(vectors, 0, hi)
             contract(unit, hi, g.at[unit, hi])
         elif unit == 1:
             contract(unit, hi, y.at[unit, hi])
@@ -180,7 +229,66 @@
             contract(unit, hi, y.at[unit, hi])
             send(unit, hi)
 
-    tabulate(1 - hi)
+    vectors = gathered(lattice)
+    tabulate(vectors, 0, 1 - hi)
+
+    def forward_lattice():
+        wait(partner, side_sem.at[1])
+        for i, c in peers():
+            pltpu.make_async_remote_copy(
+                partner, others.at[me], side_sem.at[4], side_sem.at[5],
+                device_id=plane_id(i, c), device_id_type=MESH,
+            ).start()
+        others[me] = partner[...]
+
+    def forward_raw():
+        wait(raw, side_sem.at[3])
+        hand_on(lambda i: raw.at[i // 8, :, i % 8], 1)
+
+    def tabulate_others():
+        wait(others.at[pl.ds(0, PEERS - 1)], side_sem.at[5])
+
+        @pl.when(core == hi)
+        def active():
+            vectors = gathered(others)
+            for half in (0, 1):
+                tabulate(vectors, 1, half)
+
+    def transform_joint():
+        @pl.when(core == hi)
+        def active():
+            for n in range(2):
+                wait(x.at[0, pl.ds(0, PEERS - 1)], joint_recv.at[n])
+            for half in (0, 1):
+                part = sum(
+                    jnp.dot(table[n, half], joined.at[n].reshape(1024, 128)[...], preferred_element_type=f32)
+                    for n in range(2)
+                )
+                y[JOINT, half] = part.astype(bf16).reshape(PEERS, 16, 128)
+            for i, c in peers():
+                pltpu.make_async_remote_copy(
+                    y.at[JOINT, :, i * 2 + c], joint_relayed.at[:, chip], relay_sem.at[0, 2], relay_sem.at[1, 2],
+                    device_id=plane_id(i, c), device_id_type=MESH,
+                ).start()
+            joint_relayed[:, chip] = y[JOINT, :, me]
+
+    def relay_joint():
+        pl.when(core == hi)(lambda: wait(x.at[0, pl.ds(0, 15)], relay_sem.at[1, 2]))
+        pl.when(core != hi)(lambda: wait(x.at[0, pl.ds(0, 16)], relay_sem.at[1, 2]))
+        for half in (0, 1):
+            pltpu.make_async_remote_copy(
+                joint_relayed.at[half], joint_g.at[hi], y_send.at[JOINT, half], y_recv.at[JOINT, hi],
+                device_id=z_id(half, joint_p), device_id_type=MESH,
+            ).start()
+
+    def relay(unit):
+        n = LATE.index(unit)
+        wait(x.at[0, pl.ds(0, PEERS - 1)], relay_sem.at[1, n])
+        for half in (0, 1):
+            pltpu.make_async_remote_copy(
+                relayed.at[n, half], g.at[unit, hi], y_send.at[unit, half], y_recv.at[unit, hi],
+                device_id=z_id(half, (lo + STEP[0][unit]) % 4), device_id_type=MESH,
+            ).start()
 
     def spread(unit):
         wait(g.at[unit, 1 - hi], y_recv.at[unit, 1 - hi])
@@ -189,7 +297,7 @@
         elif unit > 1:
             wait(g.at[unit, hi], y_recv.at[unit, hi])
         total = g[unit, 0].astype(f32) + g[unit, 1].astype(f32)
-        f[unit * PEERS : (unit + 1) * PEERS] = total.astype(bf16).reshape(PEERS, 16, 128)
+        f[unit * PEERS : (unit + 1) * PEERS] = total.astype(bf16)
         step = pick(STEP, core, unit)
         mode = (chip // 8) * 3 + pick(WHICH, core, unit)
         place_of = summed.at[step, mode, chip % 8]
@@ -203,13 +311,27 @@
     odd = iota((16, 128), 0) % 2 == 1
 
     def rotate(step):
+        made = [STEP[c][: LATE[0]].count(step) for c in (0, 1)]
         for c in (0, 1):
-            mine = 2 if c == step % 2 else 1
-            pl.when(core == c)(lambda: wait(f.at[pl.ds(0, 48 - mine)], f_recv.at[step]))
+            pl.when(core == c)(lambda: wait(f.at[pl.ds(0, 16 * sum(made) - made[c])], f_recv.at[step]))
+        for unit in LATE:
+            if step == STEP[0][unit]:
+                for half in (0, 1):
+                    wait(joint_g.at[half] if unit == JOINT else g.at[unit, half], y_recv.at[unit, half])
         re = (lo + 4 - step) % 4
 
         def block(b, _):
-            plain = [summed[step, k, b].astype(f32) for k in range(6)]
+            def value(k):
+                for unit in LATE:
+                    for c in (0, 1):
+                        if STEP[c][unit] == step and WHICH[c][unit] == k % 3:
+                            if unit == JOINT:
+                                return joint_g[c, k // 3 * 8 + b].astype(f32)
+                            n = (k // 3 * 8 + b) * 2 + c
+                            return g[unit, 0, n].astype(f32) + g[unit, 1, n].astype(f32)
+                return summed[step, k, b].astype(f32)
+
+            plain = [value(k) for k in range(6)]
             turned = [jnp.where(odd, pltpu.roll(v, 1, 0), -pltpu.roll(v, 15, 0)) for v in plain]
             for n in range(6):
                 total = None
@@ -222,25 +344,47 @@
 
         lax.fori_loop(0, 8, block, 0)
 
-    lag = 4
-    for unit in range(UNITS):
-        transform(unit)
-        if unit >= lag:
-            spread(unit - lag)
-    for unit in range(UNITS - lag, UNITS):
-        spread(unit)
+    transform(0)
+    transform(1)
+    forward_raw()
+    transform(2)
+    transform(3)
+    transform(4)
+    tabulate_others()
+    transform_joint()
+    spread(0)
+    relay(3)
+    spread(1)
+    relay(4)
+    relay_joint()
+    spread(2)
     wait(lattice.at[pl.ds(0, PEERS - 1)], lat_sem.at[0])
-    for unit in range(UNITS):
+    for n in range(2):
+        wait(x.at[0, pl.ds(0, PEERS - 1)], relay_sem.at[0, n])
+    pl.when(core == hi)(lambda: wait(x.at[0, pl.ds(0, PEERS - 1)], relay_sem.at[0, 2]))
+    wait(partner, side_sem.at[0])
+    wait(raw, side_sem.at[2])
+    wait(others.at[pl.ds(0, PEERS - 1)], side_sem.at[4])
+    for n in range(2):
+        pl.when(core == hi)(lambda: wait(x.at[0, pl.ds(0, 15)], joint_send.at[n]))
+        pl.when(core != hi)(lambda: wait(x.at[0, pl.ds(0, 16)], joint_send.at[n]))
+    for unit in range(JOINT):
         wait(x.at[unit, pl.ds(0, PEERS - 1)], x_send.at[unit])
+    rotate(0)
+    for unit in range(LATE[0]):
+        wait(f.at[pl.ds(0, PEERS - 1)], f_send.at[unit])
         wait(g.at[unit, 0], y_send.at[unit, 1 - hi])
         if unit == 1:
             pl.when(core == 1)(lambda: wait(g.at[unit, 0], y_send.at[unit, hi]))
         elif unit > 1:
             wait(g.at[unit, 0], y_send.at[unit, hi])
-    for step in (0, 3, 1, 2):
-        rotate(step)
-    for unit in range(UNITS):
-        wait(f.at[pl.ds(0, PEERS - 1)], f_send.at[unit])
+    rotate(3)
+    rotate(1)
+    rotate(2)
+    for half in (0, 1):
+        for unit in LATE[:2]:
+            wait(g.at[unit, 0], y_send.at[unit, half])
+        wait(joint_g.at[0], y_send.at[JOINT, half])
 
 
 def per_device(coupling, rp_coords, degeneracy, qpoints, eigvec):
@@ -260,17 +404,24 @@
             pltpu.VMEM((3, 512), jnp.int32),
             pltpu.VMEM((72, 8), jnp.float32),
             pltpu.VMEM((16, 6, 32, 2, 128), bf),
-            pltpu.VMEM((UNITS, PEERS, 16, 2, 128), bf),
+            pltpu.VMEM((JOINT, PEERS, 16, 2, 128), bf),
             pltpu.VMEM((8, 128), bf),
             pltpu.VMEM((PEERS, 8, 128), bf),
-            pltpu.VMEM((2, 512, 1024), bf),
-            pltpu.VMEM((UNITS, 2, 512, 128), bf),
-            pltpu.VMEM((UNITS, 2, 512, 128), bf),
+            pltpu.VMEM((2, 2, 512, 1024), bf),
+            pltpu.VMEM((UNITS, 2, PEERS, 16, 128), bf),
+            pltpu.VMEM((UNITS, 2, PEERS, 16, 128), bf),
             pltpu.VMEM((UNITS * PEERS, 16, 128), bf),
             pltpu.VMEM((4, 6, 8, 16, 128), bf),
             pltpu.VMEM((72, 16, 128), jnp.float32),
             pltpu.VMEM((2, 8, 512), jnp.float32),
-            dma, dma((4,)), dma((2,)), dma((UNITS,)), dma((UNITS,)),
+            pltpu.VMEM((2, 2, PEERS, 16, 128), bf),
+            pltpu.VMEM((2, PEERS, 16, 2, 128), bf),
+            pltpu.VMEM((8, 128), bf),
+            pltpu.VMEM((PEERS, 8, 128), bf),
+            pltpu.VMEM((2, 16, 8, 2, 128), bf),
+            pltpu.VMEM((2, 16, 16, 128), bf),
+            pltpu.VMEM((2, 16, 16, 128), bf),
+            dma, dma((4,)), dma((2,)), dma((2, 3)), dma((6,)), dma((2,)), dma((2,)), dma((UNITS,)), dma((UNITS,)),
             dma((UNITS, 2)), dma((UNITS, 2)), dma((UNITS,)), dma((4,)),
         ],
         compiler_params=pltpu.CompilerParams(

time: 60.8 us -> 54.5 us (0.90)
  Pallas kernels: 59.6 us -> 53.3 us
    pallas_call x1, Pallas kernels: 59.6 us -> 53.3 us  [per_device(): pl.pallas_call(exchange, out_shape=jax.ShapeDtypeStruct((8, 4, 6, 8, 2, 1...]
where the time goes in v3:
time: 54.5 us; the launch traced here: 54.4 us
  Pallas kernels  53.3 us (98%)
  local copies, waits for them, and re-layouts  1.15 us (2%)
    pallas_call x1, Pallas kernels, per_device(): pl.pallas_call(exchange, out_shape=jax.ShapeDtypeStruct((8, 4, 6, 8, 2, 1...  53.3 us
    unnamed x1, local copies, waits for them, and re-layouts  1.15 us

profile of v3, /device:TPU:1, one launch (start us, length us, event | category | flops | bytes accessed | tf_op | source)
XLA Modules:
  0.0 54.4 jit_solution(6979513719238525457)
XLA Ops:
  0.0 53.3 %exchange.1 = f32[8,4,6,8,2,128]{5,4,3,2,1,0:T(2,128)S(1)} custom-call(s32[3,16]{1,0:T(4,128)} %coords_in.1, s32[1,16]{1,0:T(1,128)} %bitcast.13, s32[3,512]{1,0:T(4,128)} %points_in.1, f32[72,8]{1,0:T(8,128)} %bitcast.12, bf16[16,6,32,2,128]{4,3,2,1,0:T(2,128)(2,1)} %bitcast.11), custom_call_target="tpu_custom_call" | custom-call | tf_op jit(solution)/shard_map/exchange/pallas_call | solution.py:396
  53.3 1.1 %copy.7 = f32[8,4,2,6,1024]{4,2,3,1,0:T(2,128)} copy(f32[8,4,2,6,1024]{4,2,3,1,0:T(2,128)S(1)} %bitcast.10) | data formatting | bytes 3145728

commit v4 on v3

--- a/solution.py
+++ b/solution.py
@@ -36,8 +36,9 @@
     return jnp.where(core == 0, table[0][unit], table[1][unit])
 
 
-def exchange(coords_in, degeneracy_in, points_in, eigvec_in, coupling, out, coords, degeneracy, points, eigvec, held, x, own, lattice, table, y, g, f, summed, coef, doubled, relayed, joined, partner, others, raw, joint_relayed, joint_g,
-             load_sem, small_sem, lat_sem, relay_sem, side_sem, joint_send, joint_recv, x_send, x_recv, y_send, y_recv, f_send, f_recv):
+def exchange(coords_in, degeneracy_in, points_in, eigvec_in, coupling, out, coords, degeneracy, points, eigvec, held, x, own, lattice, table, y, g, f, summed, coef, doubled, relayed, joined, partner, raw, joint_relayed, joint_g,
+             load_sem, small_sem, lat_send, lat_recv, raw_sem, joint_sem, relay_send, relay_recv,
+             x_send, x_recv, y_send, y_recv, f_send, f_recv):
     row, col, hi, core, lo = place()
     chip = row * 4 + col
     me = chip * 2 + core
@@ -93,22 +94,22 @@
     own[...] = jnp.where(lane // 32 == me % 4, lat, 0.0).astype(bf16)
     lattice[me] = own[...]
 
-    for i, c in peers():
-        pltpu.make_async_remote_copy(
-            own, lattice.at[me], lat_sem.at[0], lat_sem.at[1],
-            device_id=plane_id(i, c), device_id_type=MESH,
-        ).start()
     pltpu.make_async_remote_copy(
-        own, partner, side_sem.at[0], side_sem.at[1], device_id=z_id(1 - hi, lo), device_id_type=MESH
+        own, partner, lat_send, lat_recv.at[1], device_id=z_id(1 - hi, lo), device_id_type=MESH
     ).start()
     load.wait()
     joint_p = (lo + STEP[0][JOINT]) % 4
     for n in range(2):
         pltpu.make_async_remote_copy(
             held.at[:, 3 * n + pick(WHICH, 1 - hi, JOINT), pl.ds(joint_p * 8, 8)], raw.at[n],
-            side_sem.at[2], side_sem.at[3], device_id=z_id(1 - hi, lo), device_id_type=MESH,
+            raw_sem.at[0], raw_sem.at[1], device_id=z_id(1 - hi, lo), device_id_type=MESH,
         ).start()
 
+    for i, c in peers():
+        pltpu.make_async_remote_copy(
+            own, lattice.at[me], lat_send, lat_recv.at[0],
+            device_id=plane_id(i, c), device_id_type=MESH,
+        ).start()
     def piece(ref, i, c, unit):
         p = (lo + pick(STEP, c, unit)) % 4
         mode = (i // 8) * 3 + pick(WHICH, c, unit)
@@ -117,7 +118,7 @@
     def scatter(unit):
         for i, c in peers():
             pltpu.make_async_remote_copy(
-                piece(held, i, c, unit), x.at[unit, me], x_send.at[unit], x_recv.at[unit],
+                piece(held, i, c, unit), x.at[unit, me], x_send, x_recv.at[unit],
                 device_id=plane_id(i, c), device_id_type=MESH,
             ).start()
 
@@ -127,7 +128,7 @@
     def hand_on(source, n):
         def to(i):
             pltpu.make_async_remote_copy(
-                source(i), joined.at[n, me], joint_send.at[n], joint_recv.at[n],
+                source(i), joined.at[n, me], joint_sem.at[0], joint_sem.at[1],
                 device_id=plane_id(i, hi), device_id_type=MESH,
             ).start()
 
@@ -162,11 +163,11 @@
     for n in range(72):
         coef[n] = jnp.broadcast_to(columns[:, n : n + 1], (16, 128))
 
-    wait(lattice.at[pl.ds(0, PEERS - 1)], lat_sem.at[1])
-    def gathered(ref):
+    wait(lattice.at[pl.ds(0, PEERS - 1)], lat_recv.at[0])
+    def gathered(first):
         groups = []
         for n in range(PEERS // 4):
-            quad = ref[4 * n : 4 * n + 4].astype(f32)
+            quad = lattice[first + 4 * n : first + 4 * n + 4].astype(f32)
             groups.append(quad[0] + quad[1] + quad[2] + quad[3])
         return jnp.concatenate(groups, axis=1)
 
@@ -187,7 +188,7 @@
     def send(unit, half):
         p = (lo + pick(STEP, core, unit)) % 4
         pltpu.make_async_remote_copy(
-            y.at[unit, half], g.at[unit, hi], y_send.at[unit, half], y_recv.at[unit, hi],
+            y.at[unit, half], g.at[unit, hi], y_send, y_recv.at[unit],
             device_id=z_id(half, p), device_id_type=MESH,
         ).start()
 
@@ -203,7 +204,7 @@
                 contract(unit, half, y.at[unit, half])
             for i, c in peers():
                 pltpu.make_async_remote_copy(
-                    y.at[unit, :, i * 2 + c], relayed.at[n, :, me], relay_sem.at[0, n], relay_sem.at[1, n],
+                    y.at[unit, :, i * 2 + c], relayed.at[n, :, me], relay_send, relay_recv.at[n],
                     device_id=plane_id(i, c), device_id_type=MESH,
                 ).start()
             relayed[n, :, me] = y[unit, :, me]
@@ -229,36 +230,35 @@
             contract(unit, hi, y.at[unit, hi])
             send(unit, hi)
 
-    vectors = gathered(lattice)
+    vectors = gathered(0)
     tabulate(vectors, 0, 1 - hi)
 
     def forward_lattice():
-        wait(partner, side_sem.at[1])
+        wait(partner, lat_recv.at[1])
         for i, c in peers():
             pltpu.make_async_remote_copy(
-                partner, others.at[me], side_sem.at[4], side_sem.at[5],
+                partner, lattice.at[PEERS + me], lat_send, lat_recv.at[2],
                 device_id=plane_id(i, c), device_id_type=MESH,
             ).start()
-        others[me] = partner[...]
+        lattice[PEERS + me] = partner[...]
 
     def forward_raw():
-        wait(raw, side_sem.at[3])
+        wait(raw, raw_sem.at[1])
         hand_on(lambda i: raw.at[i // 8, :, i % 8], 1)
 
     def tabulate_others():
-        wait(others.at[pl.ds(0, PEERS - 1)], side_sem.at[5])
+        wait(lattice.at[pl.ds(0, PEERS - 1)], lat_recv.at[2])
 
         @pl.when(core == hi)
         def active():
-            vectors = gathered(others)
+            vectors = gathered(PEERS)
             for half in (0, 1):
                 tabulate(vectors, 1, half)
 
     def transform_joint():
         @pl.when(core == hi)
         def active():
-            for n in range(2):
-                wait(x.at[0, pl.ds(0, PEERS - 1)], joint_recv.at[n])
+            wait(x.at[pl.ds(0, 2), pl.ds(0, PEERS - 1)], joint_sem.at[1])
             for half in (0, 1):
                 part = sum(
                     jnp.dot(table[n, half], joined.at[n].reshape(1024, 128)[...], preferred_element_type=f32)
@@ -267,35 +267,37 @@
                 y[JOINT, half] = part.astype(bf16).reshape(PEERS, 16, 128)
             for i, c in peers():
                 pltpu.make_async_remote_copy(
-                    y.at[JOINT, :, i * 2 + c], joint_relayed.at[:, chip], relay_sem.at[0, 2], relay_sem.at[1, 2],
+                    y.at[JOINT, :, i * 2 + c], joint_relayed.at[:, chip], relay_send, relay_recv.at[2],
                     device_id=plane_id(i, c), device_id_type=MESH,
                 ).start()
             joint_relayed[:, chip] = y[JOINT, :, me]
 
     def relay_joint():
-        pl.when(core == hi)(lambda: wait(x.at[0, pl.ds(0, 15)], relay_sem.at[1, 2]))
-        pl.when(core != hi)(lambda: wait(x.at[0, pl.ds(0, 16)], relay_sem.at[1, 2]))
+        pl.when(core == hi)(lambda: wait(x.at[0, pl.ds(0, 15)], relay_recv.at[2]))
+        pl.when(core != hi)(lambda: wait(x.at[0, pl.ds(0, 16)], relay_recv.at[2]))
         for half in (0, 1):
             pltpu.make_async_remote_copy(
-                joint_relayed.at[half], joint_g.at[hi], y_send.at[JOINT, half], y_recv.at[JOINT, hi],
+                joint_relayed.at[half], joint_g.at[hi], y_send, y_recv.at[JOINT],
                 device_id=z_id(half, joint_p), device_id_type=MESH,
             ).start()
 
     def relay(unit):
         n = LATE.index(unit)
-        wait(x.at[0, pl.ds(0, PEERS - 1)], relay_sem.at[1, n])
+        wait(x.at[0, pl.ds(0, PEERS - 1)], relay_recv.at[n])
         for half in (0, 1):
             pltpu.make_async_remote_copy(
-                relayed.at[n, half], g.at[unit, hi], y_send.at[unit, half], y_recv.at[unit, hi],
+                relayed.at[n, half], g.at[unit, hi], y_send, y_recv.at[unit],
                 device_id=z_id(half, (lo + STEP[0][unit]) % 4), device_id_type=MESH,
             ).start()
 
     def spread(unit):
-        wait(g.at[unit, 1 - hi], y_recv.at[unit, 1 - hi])
-        if unit == 1:
-            pl.when(core == 1)(lambda: wait(g.at[unit, hi], y_recv.at[unit, hi]))
-        elif unit > 1:
-            wait(g.at[unit, hi], y_recv.at[unit, hi])
+        if unit == 0:
+            wait(g.at[unit, 0], y_recv.at[unit])
+        elif unit == 1:
+            pl.when(core == 0)(lambda: wait(g.at[unit, 0], y_recv.at[unit]))
+            pl.when(core == 1)(lambda: wait(g.at[unit], y_recv.at[unit]))
+        else:
+            wait(g.at[unit], y_recv.at[unit])
         total = g[unit, 0].astype(f32) + g[unit, 1].astype(f32)
         f[unit * PEERS : (unit + 1) * PEERS] = total.astype(bf16)
         step = pick(STEP, core, unit)
@@ -303,7 +305,7 @@
         place_of = summed.at[step, mode, chip % 8]
         for i, c in peers():
             pltpu.make_async_remote_copy(
-                f.at[unit * PEERS + i * 2 + c], place_of, f_send.at[unit], f_recv.at[step],
+                f.at[unit * PEERS + i * 2 + c], place_of, f_send, f_recv.at[step],
                 device_id=plane_id(i, c), device_id_type=MESH,
             ).start()
         place_of[...] = f[unit * PEERS + me]
@@ -316,8 +318,7 @@
             pl.when(core == c)(lambda: wait(f.at[pl.ds(0, 16 * sum(made) - made[c])], f_recv.at[step]))
         for unit in LATE:
             if step == STEP[0][unit]:
-                for half in (0, 1):
-                    wait(joint_g.at[half] if unit == JOINT else g.at[unit, half], y_recv.at[unit, half])
+                wait(joint_g if unit == JOINT else g.at[unit], y_recv.at[unit])
         re = (lo + 4 - step) % 4
 
         def block(b, _):
@@ -358,33 +359,21 @@
     relay(4)
     relay_joint()
     spread(2)
-    wait(lattice.at[pl.ds(0, PEERS - 1)], lat_sem.at[0])
-    for n in range(2):
-        wait(x.at[0, pl.ds(0, PEERS - 1)], relay_sem.at[0, n])
-    pl.when(core == hi)(lambda: wait(x.at[0, pl.ds(0, PEERS - 1)], relay_sem.at[0, 2]))
-    wait(partner, side_sem.at[0])
-    wait(raw, side_sem.at[2])
-    wait(others.at[pl.ds(0, PEERS - 1)], side_sem.at[4])
-    for n in range(2):
-        pl.when(core == hi)(lambda: wait(x.at[0, pl.ds(0, 15)], joint_send.at[n]))
-        pl.when(core != hi)(lambda: wait(x.at[0, pl.ds(0, 16)], joint_send.at[n]))
-    for unit in range(JOINT):
-        wait(x.at[unit, pl.ds(0, PEERS - 1)], x_send.at[unit])
+    wait(lattice.at[pl.ds(0, 2 * PEERS - 1)], lat_send)
+    wait(raw, raw_sem.at[0])
+    wait(x.at[:, pl.ds(0, PEERS - 1)], x_send)
+    pl.when(core == hi)(lambda: wait(x.at[pl.ds(0, 2), pl.ds(0, 15)], joint_sem.at[0]))
+    pl.when(core != hi)(lambda: wait(x.at[pl.ds(0, 2), pl.ds(0, 16)], joint_sem.at[0]))
+    pl.when(core == hi)(lambda: wait(x.at[pl.ds(0, 3), pl.ds(0, PEERS - 1)], relay_send))
+    pl.when(core != hi)(lambda: wait(x.at[pl.ds(0, 2), pl.ds(0, PEERS - 1)], relay_send))
     rotate(0)
-    for unit in range(LATE[0]):
-        wait(f.at[pl.ds(0, PEERS - 1)], f_send.at[unit])
-        wait(g.at[unit, 0], y_send.at[unit, 1 - hi])
-        if unit == 1:
-            pl.when(core == 1)(lambda: wait(g.at[unit, 0], y_send.at[unit, hi]))
-        elif unit > 1:
-            wait(g.at[unit, 0], y_send.at[unit, hi])
+    wait(f.at[pl.ds(0, LATE[0] * (PEERS - 1))], f_send)
     rotate(3)
     rotate(1)
     rotate(2)
-    for half in (0, 1):
-        for unit in LATE[:2]:
-            wait(g.at[unit, 0], y_send.at[unit, half])
-        wait(joint_g.at[0], y_send.at[JOINT, half])
+    halves = g.reshape(2 * UNITS, PEERS, 16, 128)
+    pl.when(core == 0)(lambda: wait(halves.at[pl.ds(0, 9)], y_send))
+    pl.when(core == 1)(lambda: wait(halves.at[pl.ds(0, 10)], y_send))
 
 
 def per_device(coupling, rp_coords, degeneracy, qpoints, eigvec):
@@ -406,7 +395,7 @@
             pltpu.VMEM((16, 6, 32, 2, 128), bf),
             pltpu.VMEM((JOINT, PEERS, 16, 2, 128), bf),
             pltpu.VMEM((8, 128), bf),
-            pltpu.VMEM((PEERS, 8, 128), bf),
+            pltpu.VMEM((2 * PEERS, 8, 128), bf),
             pltpu.VMEM((2, 2, 512, 1024), bf),
             pltpu.VMEM((UNITS, 2, PEERS, 16, 128), bf),
             pltpu.VMEM((UNITS, 2, PEERS, 16, 128), bf),
@@ -417,12 +406,11 @@
             pltpu.VMEM((2, 2, PEERS, 16, 128), bf),
             pltpu.VMEM((2, PEERS, 16, 2, 128), bf),
             pltpu.VMEM((8, 128), bf),
-            pltpu.VMEM((PEERS, 8, 128), bf),
             pltpu.VMEM((2, 16, 8, 2, 128), bf),
             pltpu.VMEM((2, 16, 16, 128), bf),
             pltpu.VMEM((2, 16, 16, 128), bf),
-            dma, dma((4,)), dma((2,)), dma((2, 3)), dma((6,)), dma((2,)), dma((2,)), dma((UNITS,)), dma((UNITS,)),
-            dma((UNITS, 2)), dma((UNITS, 2)), dma((UNITS,)), dma((4,)),
+            dma, dma((4,)), dma, dma((3,)), dma((2,)), dma((2,)), dma, dma((3,)),
+            dma, dma((JOINT,)), dma, dma((UNITS,)), dma, dma((4,)),
         ],
         compiler_params=pltpu.CompilerParams(
             collective_id=0, has_side_effects=True, vmem_limit_bytes=40 * 2**20

time: 54.5 us -> 54.2 us (level)
  no operation moved by 1% of the time
where the time goes in v4:
time: 54.2 us
  Pallas kernels  53 us (98%)
  local copies, waits for them, and re-layouts  1.15 us (2%)
    pallas_call x1, Pallas kernels, per_device(): pl.pallas_call(exchange, out_shape=jax.ShapeDtypeStruct((8, 4, 6, 8, 2, 1...  53 us
    unnamed x1, local copies, waits for them, and re-layouts  1.15 us

profile of v4, /device:TPU:1, one launch (start us, length us, event | category | flops | bytes accessed | tf_op | source)
XLA Modules:
  0.0 54.2 jit_solution(15530657585369784930)
XLA Ops:
  0.0 53.0 %exchange.1 = f32[8,4,6,8,2,128]{5,4,3,2,1,0:T(2,128)S(1)} custom-call(s32[3,16]{1,0:T(4,128)} %coords_in.1, s32[1,16]{1,0:T(1,128)} %bitcast.13, s32[3,512]{1,0:T(4,128)} %points_in.1, f32[72,8]{1,0:T(8,128)} %bitcast.12, bf16[16,6,32,2,128]{4,3,2,1,0:T(2,128)(2,1)} %bitcast.11), custom_call_target="tpu_custom_call" | custom-call | tf_op jit(solution)/shard_map/exchange/pallas_call | solution.py:385
  53.0 1.1 %copy.7 = f32[8,4,2,6,1024]{4,2,3,1,0:T(2,128)} copy(f32[8,4,2,6,1024]{4,2,3,1,0:T(2,128)S(1)} %bitcast.10) | data formatting | bytes 3145728

commit v5 on v4

--- a/solution.py
+++ b/solution.py
@@ -36,7 +36,7 @@
     return jnp.where(core == 0, table[0][unit], table[1][unit])
 
 
-def exchange(coords_in, degeneracy_in, points_in, eigvec_in, coupling, out, coords, degeneracy, points, eigvec, held, x, own, lattice, table, y, g, f, summed, coef, doubled, relayed, joined, partner, raw, joint_relayed, joint_g,
+def exchange(coords_in, degeneracy_in, points_in, eigvec_in, coupling, out, coords, degeneracy, points, eigvec, held, x, own, lattice, table, y, g, f, summed, coef, doubled, relayed, joined, partner, raw, joint_relayed, joint_g, so_far,
              load_sem, small_sem, lat_send, lat_recv, raw_sem, joint_sem, relay_send, relay_recv,
              x_send, x_recv, y_send, y_recv, f_send, f_recv):
     row, col, hi, core, lo = place()
@@ -312,13 +312,17 @@
 
     odd = iota((16, 128), 0) % 2 == 1
 
-    def rotate(step):
+    def arrived(step, late):
         made = [STEP[c][: LATE[0]].count(step) for c in (0, 1)]
-        for c in (0, 1):
-            pl.when(core == c)(lambda: wait(f.at[pl.ds(0, 16 * sum(made) - made[c])], f_recv.at[step]))
+        if not late:
+            for c in (0, 1):
+                pl.when(core == c)(lambda: wait(f.at[pl.ds(0, 16 * sum(made) - made[c])], f_recv.at[step]))
+            return
         for unit in LATE:
             if step == STEP[0][unit]:
                 wait(joint_g if unit == JOINT else g.at[unit], y_recv.at[unit])
+
+    def rotate(step, modes=range(6), first=True, last=True):
         re = (lo + 4 - step) % 4
 
         def block(b, _):
@@ -332,18 +336,21 @@
                             return g[unit, 0, n].astype(f32) + g[unit, 1, n].astype(f32)
                 return summed[step, k, b].astype(f32)
 
-            plain = [value(k) for k in range(6)]
-            turned = [jnp.where(odd, pltpu.roll(v, 1, 0), -pltpu.roll(v, 15, 0)) for v in plain]
+            plain = {k: value(k) for k in modes}
+            turned = {k: jnp.where(odd, pltpu.roll(v, 1, 0), -pltpu.roll(v, 15, 0)) for k, v in plain.items()}
             for n in range(6):
-                total = None
-                for k in range(6):
+                total = None if first else so_far[b, n]
+                for k in modes:
                     at = (k * 6 + n) * 2
                     term = coef[at] * plain[k] + coef[at + 1] * turned[k]
                     total = term if total is None else total + term
-                out[:, re, n, b] = total.reshape(8, 2, 128)
+                if last:
+                    out[:, re, n, b] = total.reshape(8, 2, 128)
+                else:
+                    so_far[b, n] = total
             return 0
 
-        lax.fori_loop(0, 8, block, 0)
+        lax.fori_loop(0, 8, block, 0, unroll=2)
 
     transform(0)
     transform(1)
@@ -366,11 +373,17 @@
     pl.when(core != hi)(lambda: wait(x.at[pl.ds(0, 2), pl.ds(0, 16)], joint_sem.at[0]))
     pl.when(core == hi)(lambda: wait(x.at[pl.ds(0, 3), pl.ds(0, PEERS - 1)], relay_send))
     pl.when(core != hi)(lambda: wait(x.at[pl.ds(0, 2), pl.ds(0, PEERS - 1)], relay_send))
+    arrived(0, False)
     rotate(0)
+    arrived(2, False)
+    rotate(2, (0, 3), last=False)
     wait(f.at[pl.ds(0, LATE[0] * (PEERS - 1))], f_send)
-    rotate(3)
-    rotate(1)
-    rotate(2)
+    for step in (3, 1):
+        arrived(step, False)
+        arrived(step, True)
+        rotate(step)
+    arrived(2, True)
+    rotate(2, (1, 2, 4, 5), first=False)
     halves = g.reshape(2 * UNITS, PEERS, 16, 128)
     pl.when(core == 0)(lambda: wait(halves.at[pl.ds(0, 9)], y_send))
     pl.when(core == 1)(lambda: wait(halves.at[pl.ds(0, 10)], y_send))
@@ -409,6 +422,7 @@
             pltpu.VMEM((2, 16, 8, 2, 128), bf),
             pltpu.VMEM((2, 16, 16, 128), bf),
             pltpu.VMEM((2, 16, 16, 128), bf),
+            pltpu.VMEM((8, 6, 16, 128), jnp.float32),
             dma, dma((4,)), dma, dma((3,)), dma((2,)), dma((2,)), dma, dma((3,)),
             dma, dma((JOINT,)), dma, dma((UNITS,)), dma, dma((4,)),
         ],

time: 54.2 us -> 54.1 us (level)
  no operation moved by 1% of the time
where the time goes in v5:
time: 54.1 us; the launch traced here: 54 us
  Pallas kernels  52.9 us (98%)
  local copies, waits for them, and re-layouts  1.15 us (2%)
    pallas_call x1, Pallas kernels, per_device(): pl.pallas_call(exchange, out_shape=jax.ShapeDtypeStruct((8, 4, 6, 8, 2, 1...  52.9 us
    unnamed x1, local copies, waits for them, and re-layouts  1.15 us

profile of v5, /device:TPU:1, one launch (start us, length us, event | category | flops | bytes accessed | tf_op | source)
XLA Modules:
  0.0 54.0 jit_solution(10648497174223126208)
XLA Ops:
  0.0 52.9 %exchange.1 = f32[8,4,6,8,2,128]{5,4,3,2,1,0:T(2,128)S(1)} custom-call(s32[3,16]{1,0:T(4,128)} %coords_in.1, s32[1,16]{1,0:T(1,128)} %bitcast.13, s32[3,512]{1,0:T(4,128)} %points_in.1, f32[72,8]{1,0:T(8,128)} %bitcast.12, bf16[16,6,32,2,128]{4,3,2,1,0:T(2,128)(2,1)} %bitcast.11), custom_call_target="tpu_custom_call" | custom-call | tf_op jit(solution)/shard_map/exchange/pallas_call | solution.py:398
  52.9 1.1 %copy.7 = f32[8,4,2,6,1024]{4,2,3,1,0:T(2,128)} copy(f32[8,4,2,6,1024]{4,2,3,1,0:T(2,128)S(1)} %bitcast.10) | data formatting | bytes 3145728

commit v6 on v5

--- a/solution.py
+++ b/solution.py
@@ -350,7 +350,7 @@
                     so_far[b, n] = total
             return 0
 
-        lax.fori_loop(0, 8, block, 0, unroll=2)
+        lax.fori_loop(0, 8, block, 0, unroll=4)
 
     transform(0)
     transform(1)

time: 54.1 us -> 54.1 us (level)
  no operation moved by 1% of the time
where the time goes in v6:
time: 54.1 us; the launch traced here: 54 us
  Pallas kernels  52.9 us (98%)
  local copies, waits for them, and re-layouts  1.15 us (2%)
    pallas_call x1, Pallas kernels, per_device(): pl.pallas_call(exchange, out_shape=jax.ShapeDtypeStruct((8, 4, 6, 8, 2, 1...  52.9 us
    unnamed x1, local copies, waits for them, and re-layouts  1.15 us

profile of v6, /device:TPU:1, one launch (start us, length us, event | category | flops | bytes accessed | tf_op | source)
XLA Modules:
  0.0 54.0 jit_solution(8535223530580340704)
XLA Ops:
  0.0 52.9 %exchange.1 = f32[8,4,6,8,2,128]{5,4,3,2,1,0:T(2,128)S(1)} custom-call(s32[3,16]{1,0:T(4,128)} %coords_in.1, s32[1,16]{1,0:T(1,128)} %bitcast.13, s32[3,512]{1,0:T(4,128)} %points_in.1, f32[72,8]{1,0:T(8,128)} %bitcast.12, bf16[16,6,32,2,128]{4,3,2,1,0:T(2,128)(2,1)} %bitcast.11), custom_call_target="tpu_custom_call" | custom-call | tf_op jit(solution)/shard_map/exchange/pallas_call | solution.py:398
  52.9 1.1 %copy.7 = f32[8,4,2,6,1024]{4,2,3,1,0:T(2,128)} copy(f32[8,4,2,6,1024]{4,2,3,1,0:T(2,128)S(1)} %bitcast.10) | data formatting | bytes 3145728
